TPU v7x, 256 devices: a whole 4x4x8 slice. The times are simulated.
256 devices in a mesh: row: 32 (over y, z), col: 8 (over x, core).
Axes of the slice: x: 4, y: 4, z: 8, core: 2. Of those that a mesh axis runs over, the one named last changes fastest.
Arguments:
- grams: bfloat16 [4, 3584, 3584], P(None, 'row', 'col'), as said below
- weights: bfloat16 [4, 3584, 7168], P(None, 'row', 'col'), may hold values from -6 to 6
Outputs:
- merged: float32 [3584, 7168], P('row', 'col')
- residual: float32 [3584, 7168], P('row', 'col')
Inputs may be any that keep to these rules, and one draw needn't show every extreme that they name: `grams`: each of the 4 matrices is symmetric and positive definite.
All inputs are finite; a program needn't handle non-finite values.
Results may differ from a plain program's by a relative error of at most 0.012.
The roundings to bfloat16 on the way count: a program that leaves them out, or rounds other values in their place, can miss the bound.
Values may be sent and summed in bfloat16 or wider, within the bound.
A program may use at most 256 MiB of HBM per device.

v0:
```python
import jax
import jax.numpy as jnp
from jax import lax
from jax.sharding import Mesh
from jax.sharding import PartitionSpec as P

ITERS = 2
ROW = ("row_0", "row_1")


def sum_by_axis(so_far, axes):
    for axis in axes:
        so_far = lax.psum_scatter(so_far, axis, scatter_dimension=0, tiled=True)
    return so_far


def sent_to_all(x, axis):
    copies = jnp.broadcast_to(x, (lax.axis_size(axis), *x.shape))
    return lax.all_to_all(copies, axis, split_axis=0, concat_axis=0, tiled=True)


def of_everyone(x, axis):
    return sent_to_all(x, axis).sum(axis=0)


def together(arrays, axis):
    ravelled, at, done = (jnp.concatenate([a.reshape(-1) for a in arrays]), 0, [])
    so_far = of_everyone(ravelled, axis)
    for a in arrays:
        done.append(so_far[at : at + a.size].reshape(a.shape))
        at += a.size
    return tuple(done)


def shards(grams, weights):
    slab_rows = grams.shape[1]
    col_count = weights.shape[2]
    first_row = lax.axis_index(ROW) * slab_rows
    high = lax.Precision.HIGHEST
    gram_slabs = lax.all_gather(grams, "col", axis=2, tiled=True)
    gram_total = jnp.sum(gram_slabs, axis=0, dtype=jnp.float32)
    square_block = lax.dynamic_slice_in_dim(gram_slabs, first_row, slab_rows, gram_slabs.ndim - 1)
    diag_total = jnp.einsum(
        "mr,mrc->rc",
        jnp.diagonal(square_block, axis1=-2, axis2=-1).astype(jnp.float32),
        weights.astype(jnp.float32),
    )
    product = sum_by_axis(
        jnp.einsum("mrk,mrc->kc", gram_slabs, weights, preferred_element_type=jnp.float32), ROW
    )
    right_side = 0.9 * product + 0.1 * diag_total
    total_diag = jnp.diagonal(lax.dynamic_slice_in_dim(gram_total, first_row, slab_rows, 1))
    merged = jnp.zeros((slab_rows, col_count), jnp.float32)
    residual = right_side
    direction = right_side
    for iteration in range(ITERS):
        rounded = direction.astype(jnp.bfloat16)
        shard_piece = lax.all_gather(rounded, ROW, axis=0, tiled=True)
        add_columns = lax.slice_in_dim(gram_total, 0, shard_piece.shape[0], axis=1)
        mapped = jnp.zeros((slab_rows, col_count), jnp.float32) + jnp.dot(
            add_columns, shard_piece.astype(jnp.float32), precision=high
        )
        mapped = 0.9 * mapped + 0.1 * total_diag[:, None] * rounded.astype(jnp.float32)
        curvature, cross_term, square, norm_now = together(
            (
                jnp.sum(direction * mapped, axis=0),
                jnp.sum(residual * mapped, axis=0),
                jnp.sum(mapped * mapped, axis=0),
                jnp.sum(residual * residual, axis=0),
            ),
            ROW,
        )
        step_length = norm_now / curvature
        merged = merged + step_length * direction
        residual = residual - step_length * mapped
        if iteration + 1 < ITERS:
            norm_next = (
                norm_now - 2.0 * step_length * cross_term + step_length * step_length * square
            )
            direction = residual + norm_next / norm_now * direction
    return (merged, residual)


def solution(mesh):
    torus = Mesh(mesh.devices.reshape(4, 8, mesh.shape["col"]), ("row_0", "row_1", "col"))
    in_specs = (P(None, ROW, "col"), P(None, ROW, "col"))
    out_specs = (P(ROW, "col"), P(ROW, "col"))
    return jax.shard_map(
        shards, mesh=torus, in_specs=in_specs, out_specs=out_specs, check_vma=False
    )
```

profile of v0, /device:TPU:32, one launch (start us, length us, event | category | flops | bytes accessed | tf_op | source)
XLA Modules:
  0.0 467.3 jit_solution(11836406161750740182)
XLA Ops:
  7.2 0.0 all-gather.4.cloned.1.call-start
  7.2 2.1 copy.14
  9.3 0.0 all-gather.4.cloned.1.call-update
  9.3 0.0 reduce-scatter.3.cloned.1.call-start
  9.4 35.5 %all-gather.4.cloned.1.call-done = bf16[4,112,3584]{1,2,0:T(8,128)(2,1)} async-done(((bf16[4,112,448]{1,2,0:T(8,128)(2,1)}), bf16[4,112,3584]{1,2,0:T(8,128)(2,1)}) %all-gather.4.cloned.1.call-update) | async-done | bytes 3211280 | tf_op jit(solution)/shard_map/all_gather | solution.py:40
  44.9 8.9 %convolution_bitcast_fusion = f32[3584,896]{1,0:T(8,128)} fusion(bf16[4,112,3584]{1,2,0:T(8,128)(2,1)} %all-gather.4.cloned.1.call-done, bf16[4,112,896]{2,1,0:T(8,128)(2,1)S(1)} %copy-done), kind=kOutput, calls=%fused_computation.2 | convolution fusion | flops 2877292544 | bytes 16859136 | tf_op jit(solution)/shard_map/mrk,mrc->kc/dot_general | solution.py:49
  53.7 0.0 reduce-scatter.3.cloned.1.call-update
  53.8 0.0 reduce-scatter.5.cloned.1.call-start
  53.8 119.3 %reduce-scatter.3.cloned.1.call-done = f32[896,896]{1,0:T(8,128)} async-done(((f32[3584,896]{1,0:T(8,128)}), f32[896,896]{1,0:T(8,128)}) %reduce-scatter.3.cloned.1.call-update) | async-done | bytes 3211280 | tf_op jit(solution)/shard_map/reduce_scatter | solution.py:13
  173.1 0.0 all-gather.6.cloned.1.call-start
  173.2 0.9 constant_dynamic-slice_fusion.1
  174.1 3.2 copy.15
  177.3 2.9 gather_fusion
  180.2 0.6 fusion.2
  180.8 41.3 %reduce-scatter.5.cloned.1.call-done = f32[112,896]{1,0:T(8,128)} async-done(((f32[896,896]{1,0:T(8,128)}), f32[112,896]{1,0:T(8,128)}) %reduce-scatter.5.cloned.1.call-update) | async-done | bytes 401424 | tf_op jit(solution)/shard_map/reduce_scatter | solution.py:13
  222.1 1.8 fusion.10
  223.9 0.0 all-gather.8.cloned.1.call-start
  223.9 3.0 convert_reduce_fusion
  227.0 0.1 copy.24
  227.1 1.7 gather_fusion.1
  228.8 85.2 %all-gather.6.cloned.1.call-done = bf16[3584,896]{1,0:T(8,128)(2,1)} async-done(((bf16[112,896]{1,0:T(8,128)(2,1)}), bf16[3584,896]{1,0:T(8,128)(2,1)}) %all-gather.6.cloned.1.call-update) | async-done | bytes 6422544 | tf_op jit(solution)/shard_map/all_gather | solution.py:58
  314.0 7.0 %multiply_reduce_fusion.6 = (f32[896]{0:T(1024)S(1)}, f32[896]{0:T(1024)S(1)}, f32[896]{0:T(1024)S(1)}, f32[112,896]{1,0:T(8,128)}) fusion(f32[112,896]{1,0:T(8,128)S(1)} %get-tuple-element.14, bf16[112,896]{1,0:T(8,128)(2,1)S(1)} %copy-done.1, f32[112]{0:T(128)S(1)} %broadcast_multiply_fusion, f32[112,3584]{0,1:T(8,128)S(1)} %convert_reduce_fusion, ...), kind=kOutput, calls=%fused_computation.22 | convolution fusion | flops 4316939776 | bytes 9042880 | tf_op jit(solution)/shard_map/dot_general | solution.py:60
  320.9 0.2 broadcast_in_dim.12
  321.2 21.5 %all_to_all.12 = f32[32,1,3584]{2,1,0:T(1,128)S(1)} all-to-all(f32[32,1,3584]{2,1,0:T(1,128)S(1)} %broadcast_in_dim.12), channel_id=1, replica_groups=mesh['row_0'=4,'row_1'=8,'col'=8] {'row_0','row_1'}, dimensions={0} | all-to-all | bytes 917504 | tf_op jit(solution)/shard_map/all_to_all | solution.py:19
  342.7 0.3 reduce_sum.98
  343.0 1.7 fusion.5
  344.8 84.9 %all-gather.8.cloned.1.call-done = bf16[3584,896]{1,0:T(8,128)(2,1)} async-done(((bf16[112,896]{1,0:T(8,128)(2,1)}), bf16[3584,896]{1,0:T(8,128)(2,1)}) %all-gather.8.cloned.1.call-update) | async-done | bytes 6422544 | tf_op jit(solution)/shard_map/all_gather | solution.py:58
  429.7 7.0 %multiply_reduce_fusion.3 = (f32[896]{0:T(1024)S(1)}, f32[896]{0:T(1024)S(1)}, f32[896]{0:T(1024)S(1)}, f32[896]{0:T(1024)S(1)}, f32[112,896]{1,0:T(8,128)}) fusion(f32[112,896]{1,0:T(8,128)S(1)} %get-tuple-element.10, f32[112,896]{1,0:T(8,128)S(1)} %get-tuple-element.14, f32[896]{0:T(1024)S(1)} %get-tuple-element.11, ...), kind=kOutput, calls=%fused_computation.17 | convolution fusion | flops 4317340160 | bytes 9451456 | tf_op jit(solution)/shard_map/dot_general | solution.py:60
  436.7 0.2 broadcast_in_dim.13
  437.0 21.5 %all_to_all.13 = f32[32,1,3584]{2,1,0:T(1,128)S(1)} all-to-all(f32[32,1,3584]{2,1,0:T(1,128)S(1)} %broadcast_in_dim.13), channel_id=1, replica_groups=mesh['row_0'=4,'row_1'=8,'col'=8] {'row_0','row_1'}, dimensions={0} | all-to-all | bytes 917504 | tf_op jit(solution)/shard_map/all_to_all | solution.py:19
  458.5 0.3 reduce_sum.103
  458.8 2.0 multiply_subtract_fusion
  (14 shorter events, 0.1 us)
Async XLA Ops:
  7.2 37.7 %copy-start = (bf16[4,112,896]{2,1,0:T(8,128)(2,1)S(1)}, bf16[4,112,896]{2,1,0:T(8,128)(2,1)}, u32[]{:S(2)}) copy-start(bf16[4,112,896]{2,1,0:T(8,128)(2,1)} %param.3) | copy-start | bytes 2408452
  7.2 37.7 %all-gather.4.cloned.1.call-start = ((), (), s32[]{:S(2)}) async-start(), calls=%async_computation.4 | async-start | bytes 4128768 | tf_op jit(solution)/shard_map/all_gather | solution.py:40
  9.3 163.8 %reduce-scatter.3.cloned.1.call-start = ((), (), s32[]{:S(2)}) async-start(), calls=%async_computation.5 | async-start | bytes 16056320 | tf_op jit(solution)/shard_map/reduce_scatter | solution.py:13
  53.8 168.3 %reduce-scatter.5.cloned.1.call-start = ((), (), s32[]{:S(2)}) async-start(), calls=%async_computation.6 | async-start | bytes 3612672 | tf_op jit(solution)/shard_map/reduce_scatter | solution.py:13
  173.1 140.9 %all-gather.6.cloned.1.call-start = ((), (), s32[]{:S(2)}) async-start(), calls=%async_computation.7 | async-start | bytes 6623232 | tf_op jit(solution)/shard_map/all_gather | solution.py:58
  223.9 90.1 %copy-start.1 = (bf16[112,896]{1,0:T(8,128)(2,1)S(1)}, bf16[112,896]{1,0:T(8,128)(2,1)}, u32[]{:S(2)}) copy-start(bf16[112,896]{1,0:T(8,128)(2,1)} %get-tuple-element.13) | copy-start | bytes 602116
  223.9 205.8 %all-gather.8.cloned.1.call-start = ((), (), s32[]{:S(2)}) async-start(), calls=%async_computation.8 | async-start | bytes 6623232 | tf_op jit(solution)/shard_map/all_gather | solution.py:58
Sparse Core Ops, SparseCore 0:
  9.8 34.9 all-gather.3
  53.9 119.1 reduce-scatter.2
  175.6 46.4 reduce-scatter.4
  225.1 88.8 all-gather.5
  344.9 84.7 all-gather.7
where the time goes:
time: 468 us; the launch traced here: 467 us
  waiting for transfers between devices  366 us (78%)
  blocking collectives  43.1 us (9%)
  matrix products  23.4 us (5%)
  between operations  13.9 us (3%)
  local copies, waits for them, and re-layouts  11.4 us (2%)
  other arithmetic  9.11 us (2%)
    all_gather x2, waiting for transfers between devices, shards(): shard_piece = lax.all_gather(rounded, ROW, axis=0, tiled=True)  170 us
    reduce_scatter x2, waiting for transfers between devices, sum_by_axis(): so_far = lax.psum_scatter(so_far, axis, scatter_dimension=0, tiled=True)  161 us
    all_to_all x2, blocking collectives, sent_to_all(): return lax.all_to_all(copies, axis, split_axis=0, concat_axis=0, tiled=True)  43.1 us
    all_gather x1, waiting for transfers between devices, shards(): gram_slabs = lax.all_gather(grams, 'col', axis=2, tiled=True)  35.5 us
    dot_general x2, matrix products, shards(): jnp.dot(add_columns, shard_piece.astype(jnp.float32), precision=high)  14 us
  transfers between devices with their start and end apart: 5, of which 5 were waited for; matrix products, arithmetic and copies ran while one was open for 3% of the time, Pallas kernels for 0%

commit v1 on v0

--- a/solution.py
+++ b/solution.py
@@ -55,7 +55,9 @@
     direction = right_side
     for iteration in range(ITERS):
         rounded = direction.astype(jnp.bfloat16)
-        shard_piece = lax.all_gather(rounded, ROW, axis=0, tiled=True)
+        shard_piece = jnp.concatenate(
+            lax.all_to_all(jnp.stack([rounded] * lax.axis_size(ROW)), ROW, 0, 0), axis=0
+        )
         add_columns = lax.slice_in_dim(gram_total, 0, shard_piece.shape[0], axis=1)
         mapped = jnp.zeros((slab_rows, col_count), jnp.float32) + jnp.dot(
             add_columns, shard_piece.astype(jnp.float32), precision=high

time: 468 us -> 591 us (1.26)
  blocking collectives: 43.1 us -> 192 us
  waiting for transfers between devices: 366 us -> 332 us
  starting transfers between devices: 0.2 us -> 9.08 us
    all_gather x2 -> x0, waiting for transfers between devices: 170 us -> none  [shards(): shard_piece = lax.all_gather(rounded, ROW, axis=0, tiled=True)]
    all_to_all x0 -> x1, blocking collectives: none -> 148 us  [shards(): lax.all_to_all(jnp.stack([rounded] * lax.axis_size(ROW)), ROW, 0, 0)]
    all_to_all x0 -> x1, waiting for transfers between devices: none -> 136 us  [shards(): lax.all_to_all(jnp.stack([rounded] * lax.axis_size(ROW)), ROW, 0, 0)]
    all_to_all x0 -> x1, starting transfers between devices: none -> 8.96 us  [shards(): lax.all_to_all(jnp.stack([rounded] * lax.axis_size(ROW)), ROW, 0, 0)]
  transfers between devices with their start and end apart: 5 -> 4, of which waited for: 5 -> 4; matrix products, arithmetic and copies ran while one was open for 3% -> 2% of each run, Pallas kernels for 0% -> 0%
where the time goes in v1:
time: 591 us
  waiting for transfers between devices  332 us (56%)
  blocking collectives  192 us (32%)
  matrix products  20.7 us (4%)
  local copies, waits for them, and re-layouts  15 us (3%)
  between operations  13.9 us (2%)
  starting transfers between devices  9.08 us (2%)
  other arithmetic  7.76 us (1%)
    reduce_scatter x2, waiting for transfers between devices, sum_by_axis(): so_far = lax.psum_scatter(so_far, axis, scatter_dimension=0, tiled=True)  161 us
    all_to_all x1, blocking collectives, shards(): lax.all_to_all(jnp.stack([rounded] * lax.axis_size(ROW)), ROW, 0, 0)  148 us
    all_to_all x1, waiting for transfers between devices, shards(): lax.all_to_all(jnp.stack([rounded] * lax.axis_size(ROW)), ROW, 0, 0)  136 us
    all_to_all x2, blocking collectives, sent_to_all(): return lax.all_to_all(copies, axis, split_axis=0, concat_axis=0, tiled=True)  44.4 us
    all_gather x1, waiting for transfers between devices, shards(): gram_slabs = lax.all_gather(grams, 'col', axis=2, tiled=True)  35.5 us
  transfers between devices with their start and end apart: 4, of which 4 were waited for; matrix products, arithmetic and copies ran while one was open for 2% of the time, Pallas kernels for 0%

profile of v1, /device:TPU:32, one launch (start us, length us, event | category | flops | bytes accessed | tf_op | source)
XLA Modules:
  0.0 590.8 jit_solution(7656078979529393374)
XLA Ops:
  7.2 0.0 all-gather.2.cloned.1.call-start
  7.2 2.1 copy.14
  9.3 0.0 all-gather.2.cloned.1.call-update
  9.3 0.0 reduce-scatter.3.cloned.1.call-start
  9.4 35.5 %all-gather.2.cloned.1.call-done = bf16[4,112,3584]{1,2,0:T(8,128)(2,1)} async-done(((bf16[4,112,448]{1,2,0:T(8,128)(2,1)}), bf16[4,112,3584]{1,2,0:T(8,128)(2,1)}) %all-gather.2.cloned.1.call-update) | async-done | bytes 3211280 | tf_op jit(solution)/shard_map/all_gather | solution.py:40
  44.9 8.9 %convolution_bitcast_fusion = f32[3584,896]{1,0:T(8,128)} fusion(bf16[4,112,3584]{1,2,0:T(8,128)(2,1)} %all-gather.2.cloned.1.call-done, bf16[4,112,896]{2,1,0:T(8,128)(2,1)S(1)} %copy-done), kind=kOutput, calls=%fused_computation.2 | convolution fusion | flops 2877292544 | bytes 16859136 | tf_op jit(solution)/shard_map/mrk,mrc->kc/dot_general | solution.py:49
  53.8 0.0 reduce-scatter.5.cloned.1.call-start
  53.8 119.3 %reduce-scatter.3.cloned.1.call-done = f32[896,896]{1,0:T(8,128)} async-done(((f32[3584,896]{1,0:T(8,128)}), f32[896,896]{1,0:T(8,128)}) %reduce-scatter.3.cloned.1.call-update) | async-done | bytes 3211280 | tf_op jit(solution)/shard_map/reduce_scatter | solution.py:13
  173.1 0.9 constant_dynamic-slice_fusion.1
  174.0 3.2 copy.15
  177.3 2.9 gather_fusion
  180.2 0.6 fusion.2
  180.8 41.3 %reduce-scatter.5.cloned.1.call-done = f32[112,896]{1,0:T(8,128)} async-done(((f32[896,896]{1,0:T(8,128)}), f32[112,896]{1,0:T(8,128)}) %reduce-scatter.5.cloned.1.call-update) | async-done | bytes 401424 | tf_op jit(solution)/shard_map/reduce_scatter | solution.py:13
  222.1 1.1 fusion.10
  223.2 3.2 stack.4
  226.3 9.0 %all-to-all-start = ((bf16[32,112,896]{2,1,0:T(8,128)(2,1)}), bf16[32,112,896]{2,1,0:T(8,128)(2,1)}, u32[]{:S(2)}, u32[]{:S(2)}) async-start(bf16[32,112,896]{2,1,0:T(8,128)(2,1)} %stack.4), calls=%async_computation.2 | async-start | bytes 12845056 | tf_op jit(solution)/shard_map/all_to_all | solution.py:59
  235.3 3.0 convert_reduce_fusion
  238.4 0.1 copy.24
  238.5 1.7 gather_fusion.1
  240.2 136.0 %all-to-all-done = bf16[32,112,896]{2,1,0:T(8,128)(2,1)} async-done(((bf16[32,112,896]{2,1,0:T(8,128)(2,1)}), bf16[32,112,896]{2,1,0:T(8,128)(2,1)}, u32[]{:S(2)}, u32[]{:S(2)}) %all-to-all-start) | async-done | bytes 6422560 | tf_op jit(solution)/shard_map/all_to_all | solution.py:59
  376.1 6.9 %multiply_reduce_fusion.6 = (f32[896]{0:T(1024)S(1)}, f32[896]{0:T(1024)S(1)}, f32[896]{0:T(1024)S(1)}, f32[112,896]{1,0:T(8,128)}) fusion(f32[112,896]{1,0:T(8,128)S(1)} %get-tuple-element.14, bf16[112,896]{1,0:T(8,128)(2,1)S(1)} %get-tuple-element.13, f32[112]{0:T(128)S(1)} %broadcast_multiply_fusion, f32[112,3584]{0,1:T(8,128)S(1)} %convert_reduce_fusion, ...), kind=kOutput, calls=%fused_computation.22 | convolution fusion | flops 4316939776 | bytes 9042880 | tf_op jit(solution)/shard_map/dot_general | solution.py:62
  383.1 0.2 broadcast_in_dim.12
  383.3 24.7 %all_to_all.22 = f32[32,1,3584]{2,1,0:T(1,128)S(1)} all-to-all(f32[32,1,3584]{2,1,0:T(1,128)S(1)} %broadcast_in_dim.12), channel_id=1, replica_groups=mesh['row_0'=4,'row_1'=8,'col'=8] {'row_0','row_1'}, dimensions={0} | all-to-all | bytes 917504 | tf_op jit(solution)/shard_map/all_to_all | solution.py:19
  408.1 0.3 reduce_sum.98
  408.4 1.1 fusion.5
  409.4 0.5 stack.5
  409.9 147.9 %all_to_all.23 = bf16[32,112,896]{2,1,0:T(8,128)(2,1)S(1)} all-to-all(bf16[32,112,896]{2,1,0:T(8,128)(2,1)S(1)} %stack.5), channel_id=1, replica_groups=mesh['row_0'=4,'row_1'=8,'col'=8] {'row_0','row_1'}, dimensions={0} | all-to-all | bytes 12845056 | tf_op jit(solution)/shard_map/all_to_all | solution.py:59
  557.8 4.3 multiply_reduce_fusion.3
  562.1 0.2 broadcast_in_dim.13
  562.3 19.7 %all_to_all.24 = f32[32,1,3584]{2,1,0:T(1,128)S(1)} all-to-all(f32[32,1,3584]{2,1,0:T(1,128)S(1)} %broadcast_in_dim.13), channel_id=1, replica_groups=mesh['row_0'=4,'row_1'=8,'col'=8] {'row_0','row_1'}, dimensions={0} | all-to-all | bytes 917504 | tf_op jit(solution)/shard_map/all_to_all | solution.py:19
  582.0 0.3 reduce_sum.103
  582.3 2.0 multiply_subtract_fusion
  (11 shorter events, 0.1 us)
Async XLA Ops:
  7.2 37.7 %copy-start = (bf16[4,112,896]{2,1,0:T(8,128)(2,1)S(1)}, bf16[4,112,896]{2,1,0:T(8,128)(2,1)}, u32[]{:S(2)}) copy-start(bf16[4,112,896]{2,1,0:T(8,128)(2,1)} %param.3) | copy-start | bytes 2408452
  7.2 37.7 %all-gather.2.cloned.1.call-start = ((), (), s32[]{:S(2)}) async-start(), calls=%async_computation.6 | async-start | bytes 4128768 | tf_op jit(solution)/shard_map/all_gather | solution.py:40
  9.3 163.8 %reduce-scatter.3.cloned.1.call-start = ((), (), s32[]{:S(2)}) async-start(), calls=%async_computation.7 | async-start | bytes 16056320 | tf_op jit(solution)/shard_map/reduce_scatter | solution.py:13
  53.8 168.3 %reduce-scatter.5.cloned.1.call-start = ((), (), s32[]{:S(2)}) async-start(), calls=%async_computation.8 | async-start | bytes 3612672 | tf_op jit(solution)/shard_map/reduce_scatter | solution.py:13
  226.3 149.8 %all-to-all-start = ((bf16[32,112,896]{2,1,0:T(8,128)(2,1)}), bf16[32,112,896]{2,1,0:T(8,128)(2,1)}, u32[]{:S(2)}, u32[]{:S(2)}) async-start(bf16[32,112,896]{2,1,0:T(8,128)(2,1)} %stack.4), calls=%async_computation.2 | async-start | bytes 12845056 | tf_op jit(solution)/shard_map/all_to_all | solution.py:59
Sparse Core Ops, SparseCore 0:
  9.8 34.9 all-gather.1
  53.9 119.1 reduce-scatter.2
  175.6 46.4 reduce-scatter.4
